TPU v7x, 64 devices: a 2x2x8 block of a 4x4x8 slice. The times are simulated.
64 devices in a mesh: dp: 4 (over x, y), fsdp: 16 (over z, core).
Axes of the slice: x: 2, y: 2, z: 8, core: 2. Of those that a mesh axis runs over, the one named last changes fastest.
The devices are a block of a 4x4x8 slice.
Arguments:
- hidden: bfloat16 [64, 1536, 1536], P(('dp', 'fsdp')), parts along dimension 0
- g_attn: bfloat16 [1536], P('fsdp')
- w_query: bfloat16 [1536, 1536], P('fsdp')
- w_key: bfloat16 [1536, 256], P('fsdp')
- w_value: bfloat16 [1536, 256], P('fsdp')
- w_out: bfloat16 [1536, 1536], P('fsdp')
- g_mlp: bfloat16 [1536], P('fsdp')
- w_gate: bfloat16 [1536, 8960], P('fsdp')
- w_up: bfloat16 [1536, 8960], P('fsdp')
- w_down: bfloat16 [8960, 1536], P('fsdp')
- cos_tab: float32 [1536, 64], replicated
- sin_tab: float32 [1536, 64], replicated
Outputs:
- output 1: bfloat16 [64, 1536, 1536], P(('dp', 'fsdp')), parts along dimension 0
- output 2: bfloat16 [64, 1536, 2, 128], P(('dp', 'fsdp')), parts along dimension 0
- output 3: bfloat16 [64, 1536, 2, 128], P(('dp', 'fsdp')), parts along dimension 0
There are 4 independent parts. A program takes and returns all parts, laid end to end along the dimension named above; an argument that names none is the same for every part.
All inputs are finite; a program needn't handle non-finite values.
Results may differ from a plain program's by a relative error of at most 0.0145732.
Values are sent between devices in bfloat16 or wider.
A program may use at most 768 MiB of HBM per device.

v0:
```python
import functools
import jax
import jax.numpy as jnp
from jax import lax
from jax.sharding import PartitionSpec as P

NORM_EPS = 1e-5
QUERY_BLOCK = 256


def rms_norm(rows_in, gain_vec):
    upcast = rows_in.astype(jnp.float32)
    scaled = upcast * lax.rsqrt(jnp.mean(upcast * upcast, axis=-1, keepdims=True) + NORM_EPS)
    return (scaled * gain_vec.astype(jnp.float32)).astype(jnp.bfloat16)


def apply_rope(heads_in, cos_tab, sin_tab):
    half_dim = cos_tab.shape[-1]
    upcast = heads_in.astype(jnp.float32)
    lo_half = upcast[..., :half_dim]
    hi_half = upcast[..., half_dim:]
    cos_bc = cos_tab[:, None, :]
    sin_bc = sin_tab[:, None, :]
    rotated = jnp.concatenate([lo_half * cos_bc - hi_half * sin_bc, hi_half * cos_bc + lo_half * sin_bc], axis=-1)
    return rotated.astype(jnp.bfloat16)


def causal_attention(query_grp, key_rot, value_heads):
    seq_len = query_grp.shape[1]
    head_dim = query_grp.shape[-1]
    blk_len = min(QUERY_BLOCK, seq_len)
    out_blocks = []
    for blk_start in range(0, seq_len, blk_len):
        blk_stop = blk_start + blk_len
        scores = jnp.einsum("bqkgd,bskd->bkgqs", query_grp[:, blk_start:blk_stop], key_rot[:, :blk_stop], preferred_element_type=jnp.float32) * head_dim ** -0.5
        allowed = (blk_start + jnp.arange(blk_len))[:, None] >= jnp.arange(blk_stop)[None, :]
        scores = jnp.where(allowed, scores, -jnp.inf)
        prob_bf16 = jax.nn.softmax(scores, axis=-1).astype(jnp.bfloat16)
        out_blocks.append(jnp.einsum("bkgqs,bskd->bqkgd", prob_bf16, value_heads[:, :blk_stop], preferred_element_type=jnp.float32).astype(jnp.bfloat16))
    return jnp.concatenate(out_blocks, axis=1)


def decoder_layer(hidden, g_attn, w_query, w_key, w_value, w_out, g_mlp, w_gate, w_up, w_down, cos_tab, sin_tab):
    num_seqs = hidden.shape[0]
    seq_len = hidden.shape[1]
    head_dim = 2 * cos_tab.shape[1]
    num_heads = w_query.shape[1] // head_dim
    kv_heads = w_key.shape[1] // head_dim
    normed = rms_norm(hidden, g_attn)
    query_proj = jnp.dot(normed, w_query, preferred_element_type=jnp.float32).astype(jnp.bfloat16)
    key_proj = jnp.dot(normed, w_key, preferred_element_type=jnp.float32).astype(jnp.bfloat16)
    value_proj = jnp.dot(normed, w_value, preferred_element_type=jnp.float32).astype(jnp.bfloat16)
    query_rot = apply_rope(query_proj.reshape(num_seqs, seq_len, num_heads, head_dim), cos_tab, sin_tab)
    key_rot = apply_rope(key_proj.reshape(num_seqs, seq_len, kv_heads, head_dim), cos_tab, sin_tab)
    value_heads = value_proj.reshape(num_seqs, seq_len, kv_heads, head_dim)
    query_grp = query_rot.reshape(num_seqs, seq_len, kv_heads, num_heads // kv_heads, head_dim)
    attn_heads = causal_attention(query_grp, key_rot, value_heads)
    attn_flat = attn_heads.reshape(num_seqs, seq_len, num_heads * head_dim)
    attn_proj = jnp.dot(attn_flat, w_out, preferred_element_type=jnp.float32).astype(jnp.bfloat16)
    residual = (hidden.astype(jnp.float32) + attn_proj.astype(jnp.float32)).astype(jnp.bfloat16)
    normed_mlp = rms_norm(residual, g_mlp)
    gate_proj = jnp.dot(normed_mlp, w_gate, preferred_element_type=jnp.float32).astype(jnp.bfloat16)
    up_proj = jnp.dot(normed_mlp, w_up, preferred_element_type=jnp.float32).astype(jnp.bfloat16)
    act_in = (jax.nn.silu(gate_proj.astype(jnp.float32)) * up_proj.astype(jnp.float32)).astype(jnp.bfloat16)
    mlp_out = jnp.dot(act_in, w_down, preferred_element_type=jnp.float32).astype(jnp.bfloat16)
    out_hidden = (residual.astype(jnp.float32) + mlp_out.astype(jnp.float32)).astype(jnp.bfloat16)
    return out_hidden, key_rot, value_heads


def solution(mesh):
    tok_spec = P(("dp", "fsdp"), None, None)
    cache_spec = P(("dp", "fsdp"), None, None, None)
    row_spec = P("fsdp", None)
    gain_spec = P("fsdp")
    table_spec = P(None, None)
    gather_rows = functools.partial(lax.all_gather, axis_name="fsdp", axis=0, tiled=True)

    def local_layer(hidden, g_attn, w_query, w_key, w_value, w_out, g_mlp, w_gate, w_up, w_down, cos_tab, sin_tab):
        return decoder_layer(hidden, gather_rows(g_attn), gather_rows(w_query), gather_rows(w_key), gather_rows(w_value), gather_rows(w_out), gather_rows(g_mlp), gather_rows(w_gate), gather_rows(w_up), gather_rows(w_down), cos_tab, sin_tab)

    return jax.shard_map(local_layer, mesh=mesh, in_specs=(tok_spec, gain_spec, row_spec, row_spec, row_spec, row_spec, gain_spec, row_spec, row_spec, row_spec, table_spec, table_spec), out_specs=(tok_spec, cache_spec, cache_spec), check_vma=False)
```

profile of v0, /device:TPU:21, one launch (start us, length us, event | category | flops | bytes accessed | tf_op | source)
XLA Modules:
  0.0 591.6 jit_solution(12580638509341695054)
XLA Ops:
  7.2 0.7 all-gather.6.cloned.1.call-update
  8.0 0.7 all-gather.8.cloned.1.call-update
  8.8 0.7 all-gather.12.cloned.1.call-update
  9.6 0.6 all-gather.10.cloned.1.call-update
  10.2 0.1 all-gather.14.cloned.1.call-start
  10.3 0.6 all-gather.14.cloned.1.call-update
  10.9 6.6 %copy.15 = bf16[1,1536,1536]{1,2,0:T(8,128)(2,1)} copy(bf16[1,1536,1536]{2,1,0:T(8,128)(2,1)} %param.12) | data formatting | bytes 9437184 | tf_op args[0]
  17.5 3.4 fusion.11
  20.9 0.6 dynamic-slice
  22.2 0.2 dynamic-update-slice
  22.4 0.2 dynamic-update-slice.1
  22.7 31.4 %all-reduce.2 = (bf16[1536]{0:T(1024)(128)(2,1)S(1)}, bf16[1536]{0:T(1024)(128)(2,1)}) all-reduce(bf16[1536]{0:T(1024)(128)(2,1)S(1)} %dynamic-update-slice, bf16[1536]{0:T(1024)(128)(2,1)S(1)} %dynamic-update-slice.1), channel_id=1, replica_groups=mesh['dp'=4,'fsdp'=16] {'fsdp'}, use_global_device_ids=true, to_apply=%add | all-reduce | flops 3072 | bytes 12288
  54.1 21.1 %all_gather.29 = bf16[1536,256]{1,0:T(8,128)(2,1)S(1)} all-gather(bf16[96,256]{1,0:T(8,128)(2,1)S(1)} %copy-done.7), channel_id=1, replica_groups=mesh['dp'=4,'fsdp'=16] {'fsdp'}, dimensions={0}, use_global_device_ids=true | all-gather | bytes 835584 | tf_op jit(solution)/shard_map/all_gather | solution.py:79
  75.2 3.9 convolution_convert_fusion.4
  79.1 0.2 fusion.174
  79.3 0.5 copy.51
  79.8 1.6 copy.52
  81.4 2.1 copy.17
  83.6 1.2 copy.19
  84.8 0.6 convert_element_type.237
  85.3 2.6 add_convert_fusion.1
  87.9 0.4 pad_maximum_fusion.1
  88.4 7.3 %copy.30 = bf16[1,1536,2,128]{3,2,1,0:T(2,128)(2,1)} copy(bf16[1,1536,2,128]{3,1,2,0:T(8,128)(2,1)S(1)} %pad_maximum_fusion.1) | data formatting | bytes 1572864
  95.6 20.9 %all_gather.28 = bf16[1536,256]{1,0:T(8,128)(2,1)S(1)} all-gather(bf16[96,256]{1,0:T(8,128)(2,1)S(1)} %copy-done.8), channel_id=1, replica_groups=mesh['dp'=4,'fsdp'=16] {'fsdp'}, dimensions={0}, use_global_device_ids=true | all-gather | bytes 835584 | tf_op jit(solution)/shard_map/all_gather | solution.py:79
  116.5 1.7 convolution_convert_fusion.5
  118.2 1.8 copy.31
  120.1 0.1 iota_compare_fusion.4
  120.2 0.1 iota_compare_fusion.3
  120.3 0.2 iota_compare_fusion.2
  120.5 0.3 iota_compare_fusion
  120.8 0.2 iota_compare_fusion.1
  121.0 11.5 %convolution_convert_fusion.3 = bf16[1536,1536]{0,1:T(8,128)(2,1)S(1)} fusion(bf16[1536,1536]{1,0:T(8,128)(2,1)} %all-gather.6.cloned.1.call-done, bf16[1,1536,1536]{1,2,0:T(8,128)(2,1)} %copy.15, f32[1536]{0:T(1024)S(1)} %convert_element_type.199, f32[1536]{0:T(1024)S(1)} %add_rsqrt_fusion.1), kind=kOutput, calls=%fused_computation.49 | convolution fusion | flops 7259553792 | bytes 14168064 | tf_op jit(solution)/shard_map/dot_general | solution.py:50
  132.5 1.3 convert.27
  133.9 3.1 add_convert_fusion
  137.0 5.9 %copy.20 = bf16[1,1536,12,64]{3,1,2,0:T(8,128)(2,1)} copy(bf16[1,1536,12,64]{1,3,2,0:T(8,128)(2,1)} %get-tuple-element.9) | data formatting | bytes 4718592 | tf_op jit(solution)/shard_map/convert.11
  142.9 6.1 %copy.21 = bf16[1,1536,12,64]{3,1,2,0:T(8,128)(2,1)} copy(bf16[1,1536,12,64]{1,3,2,0:T(8,128)(2,1)} %get-tuple-element.8) | data formatting | bytes 4718592 | tf_op jit(solution)/shard_map/convert.10
  149.1 2.6 fusion.50
  151.6 0.7 fusion.49
  152.3 0.7 slice-done.2
  153.0 0.1 slice-done.3
  153.1 1.6 fusion.32
  154.8 2.1 fusion.26
  156.9 0.6 copy-done.1
  157.5 1.3 fusion.31
  158.8 5.9 fusion.10
  164.7 2.0 fusion.87
  166.7 7.3 %fusion.8 = (f32[2,6,256]{2,1,0:T(8,128)S(1)}, f32[2,1280,256,6]{2,1,3,0:T(8,128)}) fusion(pred[256,1280]{0,1:T(8,128)(4,1)S(1)} %iota_compare_fusion.1, bf16[1,1536,2,6,64]{4,1,3,2,0:T(8,128)(2,1)S(1)} %bitcast.374, bf16[1,1536,2,6,64]{4,1,3,2,0:T(8,128)(2,1)S(1)} %bitcast.382, bf16[1,1536,2,64]{3,1,2,0:T(8,128)(2,1)S(1)} %get-tuple-element.10, ...), kind=kOutput, calls=%fused_computation.27 | convolution fusion | flops 1021309952 | bytes 21573632 | tf_op jit(solution)/shard_map/bqkgd,bskd->bkgqs/dot_general | solution.py:35
  174.0 1.9 fusion.21
  175.9 7.1 %fusion.9 = f32[2,6,256]{2,1,0:T(8,128)S(1)} fusion(f32[2,1024,256,6]{2,1,3,0:T(8,128)} %get-tuple-element.21, f32[2,6,256]{2,1,0:T(8,128)S(1)} %get-tuple-element.20, pred[256,1024]{0,1:T(8,128)(4,1)S(1)} %iota_compare_fusion.2), kind=kLoop, calls=%fused_computation.28 | loop fusion | flops 12579840 | bytes 12869632 | tf_op jit(solution)/shard_map/reduce_sum | solution.py:38
  183.0 8.5 %fusion.6 = (f32[2,6,256]{2,1,0:T(8,128)S(1)}, f32[2,1536,256,6]{2,1,3,0:T(8,128)}) fusion(pred[256,1536]{0,1:T(8,128)(4,1)S(1)} %iota_compare_fusion, bf16[1,1536,2,6,64]{4,1,3,2,0:T(8,128)(2,1)S(1)} %bitcast.383, bf16[1,1536,2,6,64]{4,1,3,2,0:T(8,128)(2,1)S(1)} %bitcast.375, bf16[1536,2,64]{2,0,1:T(8,128)(2,1)S(1)} %bitcast.386, ...), kind=kOutput, calls=%fused_computation.16 | convolution fusion | flops 1225257984 | bytes 24784896 | tf_op jit(solution)/shard_map/bqkgd,bskd->bkgqs/dot_general | solution.py:35
  191.5 5.6 fusion.81
  197.2 8.6 %fusion.7 = f32[2,6,256]{2,1,0:T(8,128)S(1)} fusion(f32[2,1280,256,6]{2,1,3,0:T(8,128)} %get-tuple-element.23, f32[2,6,256]{2,1,0:T(8,128)S(1)} %get-tuple-element.22, pred[256,1280]{0,1:T(8,128)(4,1)S(1)} %iota_compare_fusion.1), kind=kLoop, calls=%fused_computation.23 | loop fusion | flops 15725568 | bytes 16080896 | tf_op jit(solution)/shard_map/reduce_sum | solution.py:38
  205.8 10.2 %fusion.5 = f32[2,6,256]{2,1,0:T(8,128)S(1)} fusion(f32[2,1536,256,6]{2,1,3,0:T(8,128)} %get-tuple-element.25, f32[2,6,256]{2,1,0:T(8,128)S(1)} %get-tuple-element.24, pred[256,1536]{0,1:T(8,128)(4,1)S(1)} %iota_compare_fusion), kind=kLoop, calls=%fused_computation.12 | loop fusion | flops 18871296 | bytes 19292160 | tf_op jit(solution)/shard_map/reduce_sum | solution.py:38
  216.0 7.4 %fusion.75 = bf16[1,1536,2,6,128]{1,4,3,2,0:T(8,128)(2,1)} fusion(bf16[1,1536,2,6,128]{1,4,3,2,0:T(8,128)(2,1)} %fusion.81, f32[2,6,256]{2,1,0:T(8,128)S(1)} %fusion.21, f32[2,6,256]{2,1,0:T(8,128)S(1)} %get-tuple-element.18, f32[2,768,256,6]{2,1,3,0:T(8,128)} %copy-done, pred[256,768]{0,1:T(8,128)(4,1)S(1)} %iota_compare_fusion.3, ...), kind=kOutput, calls=%fused_computation.104 | convolution fusion | flops 616169472 | bytes 10846208 | tf_op jit(solution)/shard_map/bkgqs,bskd->bqkgd/dot_general | solution.py:39
  223.4 8.2 %fusion.99 = bf16[1,1536,2,6,128]{1,4,3,2,0:T(8,128)(2,1)} fusion(bf16[1,1536,2,6,128]{1,4,3,2,0:T(8,128)(2,1)} %fusion.75, f32[2,6,256]{2,1,0:T(8,128)S(1)} %fusion.9, f32[2,6,256]{2,1,0:T(8,128)S(1)} %get-tuple-element.20, f32[2,1024,256,6]{2,1,3,0:T(8,128)} %get-tuple-element.21, pred[256,1024]{0,1:T(8,128)(4,1)S(1)} %iota_compare_fusion.2, ...), kind=kOutput, calls=%fused_computation.112 | convolution fusion | flops 821428224 | bytes 14188544 | tf_op jit(solution)/shard_map/bkgqs,bskd->bqkgd/dot_general | solution.py:39
  231.6 9.1 %fusion.93 = bf16[1,1536,2,6,128]{1,4,3,2,0:T(8,128)(2,1)} fusion(bf16[1,1536,2,6,128]{1,4,3,2,0:T(8,128)(2,1)} %fusion.99, f32[2,6,256]{2,1,0:T(8,128)S(1)} %fusion.7, f32[2,6,256]{2,1,0:T(8,128)S(1)} %get-tuple-element.22, f32[2,1280,256,6]{2,1,3,0:T(8,128)} %get-tuple-element.23, pred[256,1280]{0,1:T(8,128)(4,1)S(1)} %iota_compare_fusion.1, ...), kind=kOutput, calls=%fused_computation.110 | convolution fusion | flops 1026686976 | bytes 17530880 | tf_op jit(solution)/shard_map/bkgqs,bskd->bqkgd/dot_general | solution.py:39
  240.7 6.4 %fusion.105 = bf16[1,1536,2,6,128]{1,4,3,2,0:T(8,128)(2,1)} fusion(bf16[1,1536,2,6,128]{1,4,3,2,0:T(8,128)(2,1)} %fusion.93, bf16[1536,2,128,1]{0,2,3,1:T(8,128)(2,1)S(1)} %bitcast.398, f32[2,6,256]{2,1,0:T(8,128)S(1)} %fusion.5, f32[2,6,256]{2,1,0:T(8,128)S(1)} %get-tuple-element.24, f32[2,1536,256,6]{2,1,3,0:T(8,128)S(1)} %bitcast.385, ...), kind=kOutput, calls=%fused_computation.114 | convolution fusion | flops 1231945728 | bytes 20865024 | tf_op jit(solution)/shard_map/bkgqs,bskd->bqkgd/dot_general | solution.py:39
  247.2 13.6 %fusion.15 = (f32[1536]{0:T(1024)S(1)}, bf16[1,1536,1536]{1,2,0:T(8,128)(2,1)}) fusion(bf16[1536,1536]{0,1:T(8,128)(2,1)} %bitcast.399, bf16[1536,1536]{1,0:T(8,128)(2,1)} %all-gather.8.cloned.1.call-done, bf16[1,1536,1536]{1,2,0:T(8,128)(2,1)} %copy.15), kind=kOutput, calls=%fused_computation.34 | convolution fusion | flops 7266630144 | bytes 18880512 | tf_op jit(solution)/shard_map/dot_general | solution.py:59
  260.8 52.3 %convolution_convert_fusion = bf16[1536,8960]{1,0:T(8,128)(2,1)} fusion(bf16[1536,8960]{1,0:T(8,128)(2,1)} %all-gather.12.cloned.1.call-done, bf16[1,1536,1536]{1,2,0:T(8,128)(2,1)} %get-tuple-element.27, f32[1536]{0:T(1024)S(1)} %copy-done.9, f32[1536]{0:T(1024)S(1)} %add_rsqrt_fusion), kind=kOutput, calls=%fused_computation.7 | convolution fusion | flops 42301784064 | bytes 59781120 | tf_op jit(solution)/shard_map/dot_general | solution.py:63
  313.1 69.5 %all-gather.10.cloned.1.call-done = bf16[1536,8960]{1,0:T(8,128)(2,1)} async-done(((bf16[96,8960]{1,0:T(8,128)(2,1)}), bf16[1536,8960]{1,0:T(8,128)(2,1)}) %all-gather.10.cloned.1.call-update) | async-done | bytes 27525136 | tf_op jit(solution)/shard_map/all_gather | solution.py:79
  382.6 62.4 %fusion.4.clone.10 = bf16[1536,8960]{1,0:T(8,128)(2,1)} fusion(bf16[1536,8960]{1,0:T(8,128)(2,1)} %convolution_convert_fusion, bf16[1536,8960]{1,0:T(8,128)(2,1)} %all-gather.10.cloned.1.call-done, bf16[1,1536,1536]{1,2,0:T(8,128)(2,1)} %get-tuple-element.27, f32[1536]{0:T(1024)S(1)} %copy-done.9, ...), kind=kOutput, calls=%fused_computation.6.clone.clone.clone.clone.clone.clone.clone.clone.clone.1 | convolution fusion | flops 42411884544 | bytes 87306240 | tf_op jit(solution)/shard_map/dot_general | solution.py:62
  445.1 80.2 %all-gather.14.cloned.1.call-done = bf16[8960,1536]{1,0:T(8,128)(2,1)} async-done(((bf16[560,1536]{1,0:T(8,128)(2,1)}), bf16[8960,1536]{1,0:T(8,128)(2,1)}) %all-gather.14.cloned.1.call-update) | async-done | bytes 27525136 | tf_op jit(solution)/shard_map/all_gather | solution.py:79
  525.3 52.9 %fusion.18 = bf16[1,1536,1536]{1,2,0:T(8,128)(2,1)} fusion(bf16[1,1536,1536]{1,2,0:T(8,128)(2,1)} %get-tuple-element.27, bf16[8960,1536]{1,0:T(8,128)(2,1)} %all-gather.14.cloned.1.call-done, bf16[1536,8960]{1,0:T(8,128)(2,1)} %fusion.4.clone.10), kind=kOutput, calls=%fused_computation.37 | convolution fusion | flops 42290380800 | bytes 64487424 | tf_op jit(solution)/shard_map/dot_general | solution.py:65
  578.2 6.6 %copy.29 = bf16[1,1536,1536]{2,1,0:T(8,128)(2,1)} copy(bf16[1,1536,1536]{1,2,0:T(8,128)(2,1)} %fusion.18) | data formatting | bytes 9437184
  (69 shorter events, 0.5 us)
Async XLA Ops:
  7.2 113.9 %all-gather.6.cloned.1.call-start = ((), (), s32[]{:S(2)}) async-start(), calls=%async_computation | async-start | bytes 5013504 | tf_op jit(solution)/shard_map/all_gather | solution.py:79
  8.0 239.2 %all-gather.8.cloned.1.call-start = ((), (), s32[]{:S(2)}) async-start(), calls=%async_computation.1 | async-start | bytes 5013504 | tf_op jit(solution)/shard_map/all_gather | solution.py:79
  8.8 252.0 %all-gather.12.cloned.1.call-start = ((), (), s32[]{:S(2)}) async-start(), calls=%async_computation.3 | async-start | bytes 29245440 | tf_op jit(solution)/shard_map/all_gather | solution.py:79
  9.6 373.1 %all-gather.10.cloned.1.call-start = ((), (), s32[]{:S(2)}) async-start(), calls=%async_computation.2 | async-start | bytes 29245440 | tf_op jit(solution)/shard_map/all_gather | solution.py:79
  10.2 515.1 %all-gather.14.cloned.1.call-start = ((), (), s32[]{:S(2)}) async-start(), calls=%async_computation.4 | async-start | bytes 29245440 | tf_op jit(solution)/shard_map/all_gather | solution.py:79
  17.5 3.4 copy-start.13
  17.5 4.7 copy-start.11
  17.5 4.9 copy-start.12
  17.5 36.6 %copy-start.7 = (bf16[96,256]{1,0:T(8,128)(2,1)S(1)}, bf16[96,256]{1,0:T(8,128)(2,1)}, u32[]{:S(2)}) copy-start(bf16[96,256]{1,0:T(8,128)(2,1)} %param.15) | copy-start | bytes 147460
  79.1 4.5 copy-start.2
  79.8 5.0 copy-start.10
  84.7 31.8 %slice-start.9 = ((s8[4718592]{0:T(1024)(128)(4,1)}), s8[4194304]{0:T(1024)(128)(4,1)S(1)}, s32[]{:S(2)}) async-start(s8[4718592]{0:T(1024)(128)(4,1)} %bitcast.388), calls=%async_computation.14 | async-start | bytes 8388608
  85.3 10.3 %copy-start.8 = (bf16[96,256]{1,0:T(8,128)(2,1)S(1)}, bf16[96,256]{1,0:T(8,128)(2,1)}, u32[]{:S(2)}) copy-start(bf16[96,256]{1,0:T(8,128)(2,1)} %param.16) | copy-start | bytes 147460
  85.3 31.2 %slice-start.10 = ((s8[4718592]{0:T(1024)(128)(4,1)}), s8[524288]{0:T(1024)(128)(4,1)S(1)}, s32[]{:S(2)}) async-start(s8[4718592]{0:T(1024)(128)(4,1)} %bitcast.388), calls=%async_computation.15 | async-start | bytes 1048576
  118.2 2.0 copy-start.4
  132.5 1.3 copy-start.3
  149.0 3.3 slice-start
  149.0 3.9 slice-start.2
  149.0 4.0 slice-start.1
  149.0 4.1 slice-start.3
  154.8 2.7 copy-start.1
  156.9 17.1 %copy-start = (f32[2,768,256,6]{2,1,3,0:T(8,128)}, f32[2,768,256,6]{2,1,3,0:T(8,128)S(1)}, u32[]{:S(2)}) copy-start(f32[2,768,256,6]{2,1,3,0:T(8,128)S(1)} %get-tuple-element.19) | copy-start | bytes 28311556
  158.8 5.9 copy-start.5
  205.8 10.2 %copy-start.6 = (bf16[1536,256]{0,1:T(8,128)(2,1)S(1)}, bf16[1536,256]{0,1:T(8,128)(2,1)}, u32[]{:S(2)}) copy-start(bf16[1536,256]{0,1:T(8,128)(2,1)} %copy-done.4) | copy-start | bytes 2359300
  223.4 17.3 %slice-start.4 = ((s8[18874368]{0:T(1024)(128)(4,1)}), s8[4194304]{0:T(1024)(128)(4,1)S(1)}, s32[]{:S(2)}) async-start(s8[18874368]{0:T(1024)(128)(4,1)} %bitcast.384), calls=%async_computation.9 | async-start | bytes 8388608
  223.4 17.3 %slice-start.5 = ((s8[18874368]{0:T(1024)(128)(4,1)}), s8[4194304]{0:T(1024)(128)(4,1)S(1)}, s32[]{:S(2)}) async-start(s8[18874368]{0:T(1024)(128)(4,1)} %bitcast.384), calls=%async_computation.10 | async-start | bytes 8388608
  223.4 17.3 %slice-start.6 = ((s8[18874368]{0:T(1024)(128)(4,1)}), s8[4194304]{0:T(1024)(128)(4,1)S(1)}, s32[]{:S(2)}) async-start(s8[18874368]{0:T(1024)(128)(4,1)} %bitcast.384), calls=%async_computation.11 | async-start | bytes 8388608
  231.6 9.1 %slice-start.7 = ((s8[18874368]{0:T(1024)(128)(4,1)}), s8[4194304]{0:T(1024)(128)(4,1)S(1)}, s32[]{:S(2)}) async-start(s8[18874368]{0:T(1024)(128)(4,1)} %bitcast.384), calls=%async_computation.12 | async-start | bytes 8388608
  231.6 9.1 %slice-start.8 = ((s8[18874368]{0:T(1024)(128)(4,1)}), s8[2097152]{0:T(1024)(128)(4,1)S(1)}, s32[]{:S(2)}) async-start(s8[18874368]{0:T(1024)(128)(4,1)} %bitcast.384), calls=%async_computation.13 | async-start | bytes 4194304
  247.1 13.6 %copy-start.9 = (f32[1536]{0:T(1024)S(1)}, f32[1536]{0:T(1024)}, u32[]{:S(2)}) copy-start(f32[1536]{0:T(1024)} %convert_element_type.237) | copy-start | bytes 18436
Sparse Core Ops, SparseCore 0:
  9.6 44.4 all-gather.5
  55.8 38.7 all-gather.7
  96.2 143.0 all-gather.11
  240.8 141.8 all-gather.9
  384.1 141.1 all-gather.13
where the time goes:
time: 600 us; the launch traced here: 592 us
  matrix products  265 us (44%)
  waiting for transfers between devices  153 us (26%)
  blocking collectives  73.4 us (12%)
  local copies, waits for them, and re-layouts  42.6 us (7%)
  other arithmetic  42.1 us (7%)
  between operations  15.1 us (3%)
    all_gather x1, waiting for transfers between devices, local_layer(): gather_rows(w_down)  80.2 us
    all_gather x1, waiting for transfers between devices, local_layer(): gather_rows(w_gate)  69.5 us
    dot_general x1, matrix products, decoder_layer(): jnp.dot(normed_mlp, w_gate, preferred_element_type=jnp.float32)  62.4 us
    dot_general x1, matrix products, decoder_layer(): jnp.dot(act_in, w_down, preferred_element_type=jnp.float32)  52.9 us
    dot_general x1, matrix products, decoder_layer(): jnp.dot(normed_mlp, w_up, preferred_element_type=jnp.float32)  52.3 us
    dot_general x6, matrix products, causal_attention(): jnp.einsum('bkgqs,bskd->bqkgd', prob_bf16, value_heads[:, :blk_stop], pre...  38.7 us
    unnamed x1, blocking collectives  31.4 us
    unnamed x63, local copies, waits for them, and re-layouts  30.3 us
  transfers between devices with their start and end apart: 5, of which 2 were waited for; matrix products, arithmetic and copies ran while one was open for 49% of the time, Pallas kernels for 0%

commit v1 on v0

v1 whole, which is shorter than its diff:
```python
import functools
import math

import jax
import jax.numpy as jnp
from jax import lax
from jax.experimental import pallas as pl
from jax.experimental.pallas import tpu as pltpu
from jax.sharding import PartitionSpec as P

EPS = 1e-5
F32 = jnp.float32
BF16 = jnp.bfloat16
MESH = pl.DeviceIdType.MESH
RATE = (1, 1)


def _dot(a, b):
    return lax.dot_general(a, b, (((1,), (0,)), ((), ())), preferred_element_type=F32)


def _dot_t(a, b):
    return lax.dot_general(a, b, (((1,), (1,)), ((), ())), preferred_element_type=F32)


def layer_kernel(cfg, x_hbm, wa_in, wo_in, wg_in, wu_in, wd_in, cos_in, sin_in,
                 out_hbm, k_hbm, v_hbm, ga, go, gg, gu, gd,
                 r, h, xb, wt, wd, ct, st, gains,
                 rz, rp, rsib, sz, sp, ssib, lsem, tsem, dsem, osem):
    n, ny, rows, drows, dim, ffn, heads, kvh, hd = cfg
    seq = x_hbm.shape[0]
    qw = heads * hd
    kw = kvh * hd
    ring = n // 2
    hops = ring - 1
    q_r, q_d = rows // 4, dim // 12
    gu_chunks, gu_tiles, tile = 5, 7, 256
    d_chunks = 3
    gcols = gu_tiles * tile
    dcols = dim // d_chunks
    n_chunk = 1 + gu_chunks + d_chunks

    d = lax.axis_index("dp")
    f = lax.axis_index("fsdp")
    x, y = d // ny, d % ny
    c = f % 2
    par = (x + y) % 2
    xp = (x + 1 - 2 * (x % 2)) * ny + y
    yp = x * ny + (y + 1 - 2 * (y % 2))
    sib = f + 1 - 2 * c
    up = (f + 2) % n
    down = (f + n - 2) % n
    dev_up, dev_dn, dev_sib = (d, up), (d, down), (d, sib)
    dev_x, dev_y = (xp, f), (yp, f)

    barrier = pltpu.get_barrier_semaphore()
    for dev in (dev_up, dev_dn, dev_sib, dev_x, dev_y):
        pl.semaphore_signal(barrier, inc=1, device_id=dev, device_id_type=MESH)
    pl.semaphore_wait(barrier, 5)

    bounce = [
        (wa_in, r.at[pl.ds(0, rows), pl.ds(0, wa_in.shape[1])], ga.at[pl.ds(rows * f, rows), :]),
        (wo_in, r.at[pl.ds(rows, rows), pl.ds(0, dim)], go.at[pl.ds(rows * f, rows), :]),
        (wg_in, r.at[pl.ds(2 * rows, rows), :], gg.at[pl.ds(rows * f, rows), :]),
        (wu_in, r.at[pl.ds(3 * rows, rows), :], gu.at[pl.ds(rows * f, rows), :]),
        (wd_in, r.at[pl.ds(4 * rows, drows), pl.ds(0, dim)], gd.at[pl.ds(drows * f, drows), :]),
    ]
    loads = [pltpu.make_async_copy(s, b, lsem.at[i]) for i, (s, b, _) in enumerate(bounce)]
    puts = [pltpu.make_async_copy(b, t, lsem.at[i]) for i, (_, b, t) in enumerate(bounce)]
    ld_x = pltpu.make_async_copy(x_hbm, xb, lsem.at[5])
    ld_c = pltpu.make_async_copy(cos_in, ct, lsem.at[6])
    ld_s = pltpu.make_async_copy(sin_in, st, lsem.at[7])

    def k_piece(buf, src, cbase, cols, idx):
        def at(f0, q):
            return buf.at[pl.ds(pl.multiple_of(rows * f0 + q_r * q, 8), q_r), pl.ds(cbase, cols)]

        def own_q(q):
            return src.at[pl.ds(pl.multiple_of(q_r * q, 8), q_r), pl.ds(cbase, cols)]

        own = src.at[:, pl.ds(cbase, cols)]
        own_dst = buf.at[pl.ds(pl.multiple_of(rows * f, 8), rows), pl.ds(cbase, cols)]
        seven = buf.at[pl.ds(0, hops * q_r), pl.ds(cbase, cols)]
        half = buf.at[pl.ds(0, ring * rows), pl.ds(cbase, cols)]
        return at, own_q, own, own_dst, seven, half, idx

    def d_piece(jd, part, idx):
        dh = drows // 2

        def col(q):
            return pl.ds(pl.multiple_of(dcols * jd + q_d * q, 128), q_d)

        def at(f0, q):
            return gd.at[pl.ds(pl.multiple_of(drows * f0 + dh * part, 8), dh), col(q)]

        def own_q(q):
            return wd_in.at[pl.ds(dh * part, dh), col(q)]

        full = pl.ds(pl.multiple_of(dcols * jd, 128), dcols)
        own = wd_in.at[pl.ds(dh * part, dh), full]
        own_dst = gd.at[pl.ds(pl.multiple_of(drows * f + dh * part, 8), dh), full]
        seven = gd.at[pl.ds(0, hops * dh), col(0)]
        half = gd.at[pl.ds(0, ring * dh), full]
        return at, own_q, own, own_dst, seven, half, idx

    def pieces_a():
        aw0 = 1152
        return [k_piece(ga, wa_in, 0, aw0, 0), k_piece(ga, wa_in, aw0, wa_in.shape[1] - aw0, 1),
                k_piece(go, wo_in, 0, dim, 2)]

    def pieces_gu(j):
        cb = pl.multiple_of(gcols * j, 128)
        return [k_piece(gg, wg_in, cb, gcols, 3 + 2 * j), k_piece(gu, wu_in, cb, gcols, 4 + 2 * j)]

    def pieces_d(jd):
        return [d_piece(jd, i, 3 + 2 * gu_chunks + 2 * jd + i) for i in range(2)]

    def rdma(src, dst, ss, rs, dev):
        return pltpu.make_async_remote_copy(src_ref=src, dst_ref=dst, send_sem=ss, recv_sem=rs,
                                            device_id=dev, device_id_type=MESH)

    def step_pieces(pieces, s):
        a = s - 1
        zs = [(0, dev_up, dev_x, (f + 2 * n - 2 * a) % n), (1, dev_dn, dev_y, (f + 2 * a) % n)]
        ax = s - 2
        xs = [(0, dev_x, (f + 2 * n - 2 * ax) % n), (1, dev_y, (f + 2 * ax) % n)]

        @pl.when(s == 1)
        def _():
            for at, own_q, own, own_dst, seven, half, i in pieces:
                for k, dev, _, _ in zs:
                    q = 2 * par + k
                    rdma(own_q(q), at(f, q), sz.at[k, i], rz.at[k, i, 0], dev).start()
                rdma(own, own_dst, ssib.at[i], rsib.at[i], dev_sib).start()

        @pl.when((s >= 2) & (s <= hops + 1))
        def _():
            for at, own_q, own, own_dst, seven, half, i in pieces:
                for k, dev, pdev, org in zs:
                    ref = at(org, 2 * par + k)
                    rdma(ref, ref, sz.at[k, i], rz.at[k, i, a - 1], dev).wait_recv()

                    @pl.when(s <= hops)
                    def _():
                        rdma(ref, ref, sz.at[k, i], rz.at[k, i, a], dev).start()

                    rdma(ref, ref, sp.at[k, i], rp.at[k, i, a - 1], pdev).start()
                    rdma(ref, ref, ssib.at[i], rsib.at[i], dev_sib).start()

        @pl.when(s >= 3)
        def _():
            for at, own_q, own, own_dst, seven, half, i in pieces:
                for k, pdev, org in xs:
                    ref = at(org, 2 * (1 - par) + k)
                    rdma(ref, ref, sp.at[k, i], rp.at[k, i, ax - 1], pdev).wait_recv()
                    rdma(ref, ref, ssib.at[i], rsib.at[i], dev_sib).start()

    def step(J, s):
        @pl.when((J >= 1) & (J <= gu_chunks))
        def _():
            step_pieces(pieces_gu(J - 1), s)

        @pl.when((J > gu_chunks) & (J < n_chunk))
        def _():
            step_pieces(pieces_d(J - 1 - gu_chunks), s)

    def pump(t, carry):
        b, k = t // 7, t % 7
        odd = k % 2

        def one(i, c2):
            step((1 - i) * (b - odd) + i * (b - 2), (1 - i) * ((k + 7 * odd) // 2 + 1) + i * (8 + k // 2))
            return c2

        return lax.fori_loop(0, 1 + (1 - odd) * ((6 - k) // 4), one, carry)

    last_pump = 7 * (n_chunk - 1) + 16

    def wait_sib(pieces):
        for at, own_q, own, own_dst, seven, half, i in pieces:
            rdma(half, half, ssib.at[i], rsib.at[i], dev_sib).wait_recv()

    for cp in loads + [ld_x, ld_c, ld_s]:
        cp.start()
    n_start = hops + 2

    def start_step(t, carry):
        step_pieces(pieces_a(), t + 1)

        @pl.when(t == 0)
        def _():
            for cp in loads:
                cp.wait()
            for cp in puts:
                cp.start()

        @pl.when(t >= 7)
        def _():
            pump(t, 0)

        return carry

    lax.fori_loop(0, n_start, start_step, 0)
    for cp in puts + [ld_x, ld_c, ld_s]:
        cp.wait()
    pcs = pieces_a()
    wait_sib(pcs[:2])

    def load_wt(src, col, width, slot, half):
        return pltpu.make_async_copy(src.at[:, pl.ds(col, width)], wt.at[slot, :, pl.ds(half * tile, width)],
                                     tsem.at[slot, half])

    aw = qw + 2 * kw
    gcp = load_wt(ga, aw, 128, 0, 0)
    gcp.start()
    gcp.wait()
    pick = (lax.broadcasted_iota(jnp.int32, (8, 128), 0) == lax.broadcasted_iota(jnp.int32, (8, 128), 1))
    gains[...] = _dot_t(pick.astype(F32).astype(BF16), wt[0, :, 0:128])

    nb = 256

    def norm(row_gain):
        def body(i, cr):
            m = pl.multiple_of(i * nb, nb)
            xv = xb[pl.ds(m, nb), :].astype(F32)
            sc = lax.rsqrt(jnp.mean(xv * xv, axis=-1, keepdims=True) + EPS)
            h[pl.ds(m, nb), :] = ((xv * sc) * gains[row_gain:row_gain + 1, :]).astype(BF16)
            return cr

        lax.fori_loop(0, seq // nb, body, 0)

    load_wt(ga, 0, 512, 0, 0).start()
    norm(0)

    mb, qb = 512, 256
    a_tiles, o_tiles, n_gu, n_d = aw // 512, dim // 512, gu_chunks * gu_tiles, dim // tile
    n_m = seq // mb
    parts = [1, 1, 1, 2, 2, 3]
    starts = [a_tiles + sum(parts[:i]) for i in range(len(parts) + 1)]
    w_o = starts[-1]
    w_g = w_o + o_tiles
    w_d = w_g + n_gu
    n_items = w_d + n_d * n_m
    group = heads // kvh
    scale = hd ** -0.5
    hpt = 512 // hd

    swap = ((lax.broadcasted_iota(jnp.int32, (hd, hd), 0) + hd // 2) % hd
            == lax.broadcasted_iota(jnp.int32, (hd, hd), 1)).astype(F32).astype(BF16)

    def rope(zb, m):
        cv, sv = ct[pl.ds(m, mb), :], st[pl.ds(m, mb), :]
        return (zb.astype(F32) * cv + _dot(zb, swap) * sv).astype(BF16)

    def qkv_tile(t, is_kv):
        slot = t % 2

        @pl.when(t + 1 < a_tiles)
        def _():
            load_wt(ga, pl.multiple_of((t + 1) * 512, 512), 512, 1 - slot, 0).start()

        load_wt(ga, 0, 512, slot, 0).wait()

        def body(i, cr):
            m = pl.multiple_of(i * mb, mb)
            z = _dot(h[pl.ds(m, mb), :], wt[slot]).astype(BF16)
            for j in range(hpt):
                zj = z[:, j * hd:(j + 1) * hd]
                if not (is_kv and j >= kvh):
                    zj = rope(zj, m)
                r[pl.ds(m, mb), pl.ds(pl.multiple_of((t * hpt + j) * hd, hd), hd)] = zj
            return cr

        lax.fori_loop(0, n_m, body, 0)

    st_k = pltpu.make_async_copy(r.at[:, pl.ds(qw, kw)], k_hbm, osem.at[0])
    st_v = pltpu.make_async_copy(r.at[:, pl.ds(qw + kw, kw)], v_hbm, osem.at[1])

    def attend(b, g):
        lo = b * qb
        cnt = heads // parts[b]
        tri = (lax.broadcasted_iota(jnp.int32, (qb, qb), 0) >= lax.broadcasted_iota(jnp.int32, (qb, qb), 1))

        def one_head(i, cr):
            head = g * cnt + i
            kv = head // group
            q = r[lo:lo + qb, pl.ds(pl.multiple_of(head * hd, hd), hd)]
            kcol = pl.ds(pl.multiple_of(qw + kv * hd, hd), hd)
            vcol = pl.ds(pl.multiple_of(qw + kw + kv * hd, hd), hd)
            s2 = jnp.where(tri, _dot_t(q, r[lo:lo + qb, kcol]), -jnp.inf)
            m = jnp.max(s2, axis=-1, keepdims=True)
            if b:
                s1 = _dot_t(q, r[0:lo, kcol])
                m = jnp.maximum(m, jnp.max(s1, axis=-1, keepdims=True))
                e1 = jnp.exp((s1 - m) * scale)
            e2 = jnp.exp((s2 - m) * scale)
            tot = jnp.sum(e2, axis=-1, keepdims=True)
            if b:
                tot = tot + jnp.sum(e1, axis=-1, keepdims=True)
            inv = 1.0 / tot
            o = _dot((e2 * inv).astype(BF16), r[lo:lo + qb, vcol])
            if b:
                o = o + _dot((e1 * inv).astype(BF16), r[0:lo, vcol])
            r[lo:lo + qb, pl.ds(pl.multiple_of(aw + head * hd, hd), hd)] = o.astype(BF16)
            return cr

        lax.fori_loop(0, cnt, one_head, 0)

    def o_tile(t):
        slot = t % 2

        @pl.when(t + 1 < o_tiles)
        def _():
            load_wt(go, pl.multiple_of((t + 1) * 512, 512), 512, 1 - slot, 0).start()

        load_wt(go, 0, 512, slot, 0).wait()
        cols = pl.ds(pl.multiple_of(t * 512, 512), 512)

        def body(i, cr):
            m = pl.multiple_of(i * mb, mb)
            a = _dot(r[pl.ds(m, mb), pl.ds(aw, qw)], wt[slot]).astype(BF16).astype(F32)
            xb[pl.ds(m, mb), cols] = (xb[pl.ds(m, mb), cols].astype(F32) + a).astype(BF16)
            return cr

        lax.fori_loop(0, n_m, body, 0)

    def load_gu(t, slot):
        cb = pl.multiple_of(t * tile, tile)
        return [load_wt(gg, cb, tile, slot, 0), load_wt(gu, cb, tile, slot, 1)]

    def fetch_gu(t):
        @pl.when(t % gu_tiles == 0)
        def _():
            wait_sib(pieces_gu(t // gu_tiles))

        for cp in load_gu(t, t % 2):
            cp.start()

    def gu_tile(t):
        slot = t % 2
        for cp in load_gu(t, slot):
            cp.wait()

        @pl.when(t + 1 < n_gu)
        def _():
            fetch_gu(t + 1)

        def body(i, c2):
            m = pl.multiple_of(i * mb, mb)
            z = _dot(h[pl.ds(m, mb), :], wt[slot])
            g = z[:, :tile].astype(BF16).astype(F32)
            u = z[:, tile:].astype(BF16).astype(F32)
            r[pl.ds(m, mb), pl.ds(pl.multiple_of(t * tile, tile), tile)] = (g / (1.0 + jnp.exp(-g)) * u).astype(BF16)
            return c2

        lax.fori_loop(0, n_m, body, 0)

    dt = dcols // tile

    def load_d(t):
        return pltpu.make_async_copy(gd.at[:, pl.ds(pl.multiple_of(t * tile, tile), tile)], wd.at[t % 2],
                                     dsem.at[t % 2])

    def store_d(t):
        cols = pl.ds(pl.multiple_of(t * tile, tile), tile)
        return pltpu.make_async_copy(xb.at[:, cols], out_hbm.at[:, cols], osem.at[2 + t])

    def d_item(i):
        t, mi = i // n_m, i % n_m

        @pl.when(mi == 0)
        def _():
            @pl.when(t % dt == 0)
            def _():
                wait_sib(pieces_d(t // dt))
                load_d(t).start()

            @pl.when(t % dt != dt - 1)
            def _():
                load_d(t + 1).start()

            load_d(t).wait()

        m = pl.multiple_of(mi * mb, mb)
        mm = _dot(r[pl.ds(m, mb), :], wd[t % 2]).astype(BF16).astype(F32)
        cols = pl.ds(pl.multiple_of(t * tile, tile), tile)
        xb[pl.ds(m, mb), cols] = (xb[pl.ds(m, mb), cols].astype(F32) + mm).astype(BF16)

        @pl.when(mi == n_m - 1)
        def _():
            store_d(t).start()

    def pumps_before(w):
        flat = jnp.minimum(w, w_g)
        up_ = jnp.minimum(jnp.maximum(w - w_g, 0), n_gu)
        rest = jnp.maximum(w - w_d, 0)
        return jnp.minimum(n_start + flat + (up_ * RATE[0]) // RATE[1] + rest, last_pump + 1)

    def item(w, carry):
        lax.fori_loop(pumps_before(w), pumps_before(w + 1), pump, 0)

        @pl.when(w < a_tiles - 1)
        def _():
            qkv_tile(w, False)

        @pl.when(w == a_tiles - 1)
        def _():
            qkv_tile(w, True)
            st_k.start()
            st_v.start()

        for b in range(len(parts)):
            @pl.when((w >= starts[b]) & (w < starts[b + 1]))
            def _(b=b):
                attend(b, w - starts[b])

        @pl.when(w == w_o)
        def _():
            wait_sib(pcs[2:])
            load_wt(go, 0, 512, 0, 0).start()

        @pl.when((w >= w_o) & (w < w_g))
        def _():
            o_tile(w - w_o)

        @pl.when(w == w_g)
        def _():
            st_k.wait()
            st_v.wait()
            fetch_gu(0)
            norm(1)

        @pl.when((w >= w_g) & (w < w_d))
        def _():
            gu_tile(w - w_g)

        @pl.when(w >= w_d)
        def _():
            d_item(w - w_d)

        return carry

    lax.fori_loop(0, n_items, item, 0)
    lax.fori_loop(0, n_d, lambda t, c2: (store_d(t).wait(), c2)[1], 0)

    def drain(pieces):
        for at, own_q, own, own_dst, seven, half, i in pieces:
            for k in range(2):
                rdma(seven, seven, sz.at[k, i], rz.at[k, i, 0], dev_up).wait_send()
                rdma(seven, seven, sp.at[k, i], rp.at[k, i, 0], dev_x).wait_send()
            rdma(half, half, ssib.at[i], rsib.at[i], dev_sib).wait_send()

    drain(pcs)
    lax.fori_loop(0, gu_chunks, lambda j, c2: (drain(pieces_gu(j)), c2)[1], 0)
    lax.fori_loop(0, d_chunks, lambda j, c2: (drain(pieces_d(j)), c2)[1], 0)


def solution(mesh):
    n = mesh.shape["fsdp"]
    ny = math.isqrt(mesh.shape["dp"])
    tok = P(("dp", "fsdp"), None, None)
    cache = P(("dp", "fsdp"), None, None, None)
    row, vec, tab = P("fsdp", None), P("fsdp"), P(None, None)

    def local(hidden, g_attn, w_query, w_key, w_value, w_out, g_mlp, w_gate, w_up, w_down, cos_tab, sin_tab):
        _, seq, dim = hidden.shape
        hd = 2 * cos_tab.shape[1]
        heads, kvh = w_query.shape[1] // hd, w_key.shape[1] // hd
        rows, ffn = w_gate.shape
        drows = w_down.shape[0]
        kw = kvh * hd
        gcol = jnp.pad(jnp.stack([g_attn, g_mlp], axis=1), ((0, 0), (0, 126)))
        wa = jnp.concatenate([w_query, w_key, w_value, gcol], axis=1)
        cos2 = jnp.concatenate([cos_tab, cos_tab], axis=1)
        sin2 = jnp.concatenate([-sin_tab, sin_tab], axis=1)
        cfg = (n, ny, rows, drows, dim, ffn, heads, kvh, hd)
        np_ = 19
        hops = n // 2 - 1
        hbm = pl.BlockSpec(memory_space=pl.ANY)
        sh = jax.ShapeDtypeStruct
        dma = pltpu.SemaphoreType.DMA
        outs = pl.pallas_call(
            functools.partial(layer_kernel, cfg),
            out_shape=[
                sh((seq, dim), BF16), sh((seq, kw), BF16), sh((seq, kw), BF16),
                sh((rows * n, wa.shape[1]), BF16), sh((rows * n, dim), BF16),
                sh((rows * n, ffn), BF16), sh((rows * n, ffn), BF16), sh((drows * n, dim), BF16),
            ],
            in_specs=[hbm] * 8,
            out_specs=[hbm] * 8,
            scratch_shapes=[
                pltpu.VMEM((seq, ffn), BF16), pltpu.VMEM((seq, dim), BF16), pltpu.VMEM((seq, dim), BF16),
                pltpu.VMEM((2, dim, 512), BF16), pltpu.VMEM((2, ffn, 256), BF16),
                pltpu.VMEM((seq, hd), F32), pltpu.VMEM((seq, hd), F32), pltpu.VMEM((8, dim), F32),
                dma((2, np_, hops)), dma((2, np_, hops)), dma((np_,)),
                dma((2, np_)), dma((2, np_)), dma((np_,)),
                dma((8,)), dma((2, 2)), dma((2,)), dma((8,)),
            ],
            compiler_params=pltpu.CompilerParams(collective_id=0, has_side_effects=True,
                                                 vmem_limit_bytes=67043328),
            name="layer",
        )(hidden[0], wa, w_out, w_gate, w_up, w_down, cos2, sin2)
        out, k, v = outs[:3]
        return out[None], k.reshape(1, seq, kvh, hd), v.reshape(1, seq, kvh, hd)

    return jax.shard_map(local, mesh=mesh,
                         in_specs=(tok, vec, row, row, row, row, vec, row, row, row, tab, tab),
                         out_specs=(tok, cache, cache), check_vma=False)
```

time: 600 us -> 358 us (0.60); the launches traced: 592 us -> 358 us
  Pallas kernels: 0 us -> 339 us
  matrix products: 265 us -> 0 us
  waiting for transfers between devices: 153 us -> 0 us
  blocking collectives: 73.4 us -> 0 us
  other arithmetic: 42.1 us -> 5.13 us
  local copies, waits for them, and re-layouts: 42.6 us -> 13.2 us
  between operations: 15.1 us -> 0.67 us
    pallas_call x0 -> x1, Pallas kernels: none -> 339 us  [local(): pl.pallas_call(functools.partial(layer_kernel, cfg), out_shape=[sh((seq,...]
    dot_general x19 -> x0, matrix products: 265 us -> none  [the longest x1 62.4 us: decoder_layer(): jnp.dot(normed_mlp, w_gate, preferred_element_type=jnp.float32)]
    all_gather x5 -> x0, waiting for transfers between devices: 150 us -> none  [the longest x1 80.2 us: local_layer(): gather_rows(w_down)]
    all_gather x2 -> x0, blocking collectives: 42 us -> none  [the longest x1 21.1 us: local_layer(): gather_rows(w_key)]
    reduce_sum x7 -> x0, other arithmetic: 33.2 us -> none  [the longest x6 29.8 us: causal_attention(): prob_bf16 = jax.nn.softmax(scores, axis=-1).astype(jnp.bfloat16)]
    unnamed x1 -> x0, blocking collectives: 31.4 us -> none
    unnamed x63 -> x3, local copies, waits for them, and re-layouts: 30.3 us -> 7.35 us
    another operation x2 -> x1, local copies, waits for them, and re-layouts: 12.1 us -> 0.13 us  [local(): gcol = jnp.pad(jnp.stack([g_attn, g_mlp], axis=1), ((0, 0), (0, 126)))]
  transfers between devices with their start and end apart: 5 -> 0, of which waited for: 2 -> 0; matrix products, arithmetic and copies ran while one was open for 49% -> 0% of each run, Pallas kernels for 0% -> 0%
where the time goes in v1:
time: 358 us
  Pallas kernels  339 us (95%)
  local copies, waits for them, and re-layouts  13.2 us (4%)
  other arithmetic  5.13 us (1%)
    pallas_call x1, Pallas kernels, local(): pl.pallas_call(functools.partial(layer_kernel, cfg), out_shape=[sh((seq,...  339 us
    unnamed x3, local copies, waits for them, and re-layouts  7.35 us

profile of v1, /device:TPU:21, one launch (start us, length us, event | category | flops | bytes accessed | tf_op | source)
XLA Modules:
  0.0 357.6 jit_solution(1901325441687199340)
XLA Ops:
  0.6 0.7 pad_maximum_fusion.2
  1.3 0.1 copy.26
  1.4 1.8 fusion.1.wa_in
  3.2 1.0 neg.3
  4.3 0.3 copy.29
  4.5 1.3 copy.27
  5.8 1.3 copy.30
  7.1 1.6 pad_maximum_fusion
  8.7 338.6 %layer.1 = (bf16[1536,1536]{1,0:T(8,128)(2,1)}, bf16[1536,256]{1,0:T(8,128)(2,1)}, bf16[1536,256]{1,0:T(8,128)(2,1)}, bf16[1536,2176]{1,0:T(8,128)(2,1)}, bf16[1...) custom-call(bf16[1536,1536]{1,0:T(8,128)(2,1)} %bitcast.5, ...), custom_call_target="tpu_custom_call" | custom-call | tf_op jit(solution)/shard_map/layer/pallas_call | solution.py:482
  347.3 2.7 reshape.12
  350.1 2.7 reshape.13
  352.8 4.8 %copy.32 = bf16[1,1536,1536]{2,1,0:T(8,128)(2,1)} copy(bf16[1,1536,1536]{2,1,0:T(8,128)(2,1)} %bitcast.4) | data formatting | bytes 9437184

commit v2 on v1

--- a/solution.py
+++ b/solution.py
@@ -13,6 +13,8 @@
 BF16 = jnp.bfloat16
 MESH = pl.DeviceIdType.MESH
 RATE = (1, 1)
+STACK = 3
+MB = 1536
 
 
 def _dot(a, b):
@@ -24,7 +26,7 @@
 
 
 def layer_kernel(cfg, x_hbm, wa_in, wo_in, wg_in, wu_in, wd_in, cos_in, sin_in,
-                 out_hbm, k_hbm, v_hbm, ga, go, gg, gu, gd,
+                 out_hbm, k_hbm, v_hbm, ga, go, gu, gd,
                  r, h, xb, wt, wd, ct, st, gains,
                  rz, rp, rsib, sz, sp, ssib, lsem, tsem, dsem, osem):
     n, ny, rows, drows, dim, ffn, heads, kvh, hd = cfg
@@ -61,8 +63,8 @@
     bounce = [
         (wa_in, r.at[pl.ds(0, rows), pl.ds(0, wa_in.shape[1])], ga.at[pl.ds(rows * f, rows), :]),
         (wo_in, r.at[pl.ds(rows, rows), pl.ds(0, dim)], go.at[pl.ds(rows * f, rows), :]),
-        (wg_in, r.at[pl.ds(2 * rows, rows), :], gg.at[pl.ds(rows * f, rows), :]),
-        (wu_in, r.at[pl.ds(3 * rows, rows), :], gu.at[pl.ds(rows * f, rows), :]),
+        (wg_in, r.at[pl.ds(2 * rows, rows), :], gu.at[0, pl.ds(rows * f, rows), :]),
+        (wu_in, r.at[pl.ds(3 * rows, rows), :], gu.at[1, pl.ds(rows * f, rows), :]),
         (wd_in, r.at[pl.ds(4 * rows, drows), pl.ds(0, dim)], gd.at[pl.ds(drows * f, drows), :]),
     ]
     loads = [pltpu.make_async_copy(s, b, lsem.at[i]) for i, (s, b, _) in enumerate(bounce)]
@@ -84,36 +86,40 @@
         half = buf.at[pl.ds(0, ring * rows), pl.ds(cbase, cols)]
         return at, own_q, own, own_dst, seven, half, idx
 
-    def d_piece(jd, part, idx):
-        dh = drows // 2
-
+    def d_piece(jd, idx):
         def col(q):
             return pl.ds(pl.multiple_of(dcols * jd + q_d * q, 128), q_d)
 
         def at(f0, q):
-            return gd.at[pl.ds(pl.multiple_of(drows * f0 + dh * part, 8), dh), col(q)]
-
-        def own_q(q):
-            return wd_in.at[pl.ds(dh * part, dh), col(q)]
+            return gd.at[pl.ds(pl.multiple_of(drows * f0, 8), drows), col(q)]
 
         full = pl.ds(pl.multiple_of(dcols * jd, 128), dcols)
-        own = wd_in.at[pl.ds(dh * part, dh), full]
-        own_dst = gd.at[pl.ds(pl.multiple_of(drows * f + dh * part, 8), dh), full]
-        seven = gd.at[pl.ds(0, hops * dh), col(0)]
-        half = gd.at[pl.ds(0, ring * dh), full]
-        return at, own_q, own, own_dst, seven, half, idx
+        own = gd.at[pl.ds(pl.multiple_of(drows * f, 8), drows), full]
+        seven = gd.at[pl.ds(0, hops * drows), col(0)]
+        half = gd.at[pl.ds(0, ring * drows), full]
+        return at, functools.partial(at, f), own, own, seven, half, idx
 
     def pieces_a():
         aw0 = 1152
         return [k_piece(ga, wa_in, 0, aw0, 0), k_piece(ga, wa_in, aw0, wa_in.shape[1] - aw0, 1),
                 k_piece(go, wo_in, 0, dim, 2)]
 
+    def gu_piece(j, idx):
+        cols = pl.ds(pl.multiple_of(gcols * j, 128), gcols)
+
+        def at(f0, q):
+            return gu.at[:, pl.ds(pl.multiple_of(rows * f0 + q_r * q, 8), q_r), cols]
+
+        own = gu.at[:, pl.ds(pl.multiple_of(rows * f, 8), rows), cols]
+        seven = gu.at[:, pl.ds(0, hops * q_r), cols]
+        half = gu.at[:, pl.ds(0, ring * rows), cols]
+        return at, functools.partial(at, f), own, own, seven, half, idx
+
     def pieces_gu(j):
-        cb = pl.multiple_of(gcols * j, 128)
-        return [k_piece(gg, wg_in, cb, gcols, 3 + 2 * j), k_piece(gu, wu_in, cb, gcols, 4 + 2 * j)]
+        return [gu_piece(j, 3 + j)]
 
     def pieces_d(jd):
-        return [d_piece(jd, i, 3 + 2 * gu_chunks + 2 * jd + i) for i in range(2)]
+        return [d_piece(jd, 3 + gu_chunks + jd)]
 
     def rdma(src, dst, ss, rs, dev):
         return pltpu.make_async_remote_copy(src_ref=src, dst_ref=dst, send_sem=ss, recv_sem=rs,
@@ -165,16 +171,16 @@
             step_pieces(pieces_d(J - 1 - gu_chunks), s)
 
     def pump(t, carry):
-        b, k = t // 7, t % 7
-        odd = k % 2
-
-        def one(i, c2):
-            step((1 - i) * (b - odd) + i * (b - 2), (1 - i) * ((k + 7 * odd) // 2 + 1) + i * (8 + k // 2))
+        lane, i = (t - 7) % 2, (t - 7) // 2
+        J, s = 1 + 2 * (i // 7) + lane, i % 7 + 1
+
+        def one(e, c2):
+            step(J - 2 * e, s + 7 * e)
             return c2
 
-        return lax.fori_loop(0, 1 + (1 - odd) * ((6 - k) // 4), one, carry)
-
-    last_pump = 7 * (n_chunk - 1) + 16
+        return lax.fori_loop(0, 1 + (9 - s) // 7, one, carry)
+
+    last_pump = 7 + (n_chunk - 2) % 2 + 2 * (7 * ((n_chunk - 2) // 2 + 1) + 1)
 
     def wait_sib(pieces):
         for at, own_q, own, own_dst, seven, half, i in pieces:
@@ -194,6 +200,11 @@
             for cp in puts:
                 cp.start()
 
+        @pl.when(t == 7)
+        def _():
+            for cp in puts:
+                cp.wait()
+
         @pl.when(t >= 7)
         def _():
             pump(t, 0)
@@ -201,7 +212,7 @@
         return carry
 
     lax.fori_loop(0, n_start, start_step, 0)
-    for cp in puts + [ld_x, ld_c, ld_s]:
+    for cp in [ld_x, ld_c, ld_s]:
         cp.wait()
     pcs = pieces_a()
     wait_sib(pcs[:2])
@@ -232,21 +243,24 @@
     load_wt(ga, 0, 512, 0, 0).start()
     norm(0)
 
-    mb, qb = 512, 256
+    mb, qb = MB, 256
     a_tiles, o_tiles, n_gu, n_d = aw // 512, dim // 512, gu_chunks * gu_tiles, dim // tile
     n_m = seq // mb
-    parts = [1, 1, 1, 2, 2, 3]
+    db = 512
+    n_dm = seq // db
+    parts = [1, 1, 1, 2, 2, 4]
     starts = [a_tiles + sum(parts[:i]) for i in range(len(parts) + 1)]
     w_o = starts[-1]
     w_g = w_o + o_tiles
     w_d = w_g + n_gu
-    n_items = w_d + n_d * n_m
+    n_items = w_d + n_d * n_dm
     group = heads // kvh
     scale = hd ** -0.5
     hpt = 512 // hd
 
-    swap = ((lax.broadcasted_iota(jnp.int32, (hd, hd), 0) + hd // 2) % hd
-            == lax.broadcasted_iota(jnp.int32, (hd, hd), 1)).astype(F32).astype(BF16)
+    row_i = lax.broadcasted_iota(jnp.int32, (hd, hd), 0)
+    col_i = lax.broadcasted_iota(jnp.int32, (hd, hd), 1)
+    swap = ((row_i + hd // 2 == col_i).astype(F32) - (row_i == col_i + hd // 2).astype(F32)).astype(BF16)
 
     def rope(zb, m):
         cv, sv = ct[pl.ds(m, mb), :], st[pl.ds(m, mb), :]
@@ -268,7 +282,14 @@
                 zj = z[:, j * hd:(j + 1) * hd]
                 if not (is_kv and j >= kvh):
                     zj = rope(zj, m)
-                r[pl.ds(m, mb), pl.ds(pl.multiple_of((t * hpt + j) * hd, hd), hd)] = zj
+                head = t * hpt + j
+                if is_kv:
+                    r[pl.ds(m, mb), pl.ds(pl.multiple_of(head * hd, hd), hd)] = zj
+                    continue
+                for e in range(mb // qb):
+                    col = ((head // group) * (seq // qb) + i * (mb // qb) + e) * hd
+                    r[pl.ds(pl.multiple_of((head % group) * qb, qb), qb), pl.ds(pl.multiple_of(col, hd), hd)] = (
+                        zj[e * qb:(e + 1) * qb])
             return cr
 
         lax.fori_loop(0, n_m, body, 0)
@@ -278,13 +299,16 @@
 
     def attend(b, g):
         lo = b * qb
-        cnt = heads // parts[b]
-        tri = (lax.broadcasted_iota(jnp.int32, (qb, qb), 0) >= lax.broadcasted_iota(jnp.int32, (qb, qb), 1))
-
-        def one_head(i, cr):
-            head = g * cnt + i
-            kv = head // group
-            q = r[lo:lo + qb, pl.ds(pl.multiple_of(head * hd, hd), hd)]
+        n_st = heads // STACK
+        cnt = n_st // parts[b]
+        per = group // STACK
+        sq = STACK * qb
+        tri = (lax.broadcasted_iota(jnp.int32, (sq, qb), 0) % qb >= lax.broadcasted_iota(jnp.int32, (sq, qb), 1))
+
+        def heads_at(i, cr):
+            unit = g * cnt + i
+            kv, part = unit // per, unit % per
+            q = r[pl.ds(pl.multiple_of(part * sq, sq), sq), pl.ds(pl.multiple_of((kv * (seq // qb) + b) * hd, hd), hd)]
             kcol = pl.ds(pl.multiple_of(qw + kv * hd, hd), hd)
             vcol = pl.ds(pl.multiple_of(qw + kw + kv * hd, hd), hd)
             s2 = jnp.where(tri, _dot_t(q, r[lo:lo + qb, kcol]), -jnp.inf)
@@ -292,19 +316,21 @@
             if b:
                 s1 = _dot_t(q, r[0:lo, kcol])
                 m = jnp.maximum(m, jnp.max(s1, axis=-1, keepdims=True))
-                e1 = jnp.exp((s1 - m) * scale)
-            e2 = jnp.exp((s2 - m) * scale)
-            tot = jnp.sum(e2, axis=-1, keepdims=True)
+            ms = m * scale
+            tot = jnp.sum(jnp.exp(s2 * scale - ms), axis=-1, keepdims=True)
             if b:
-                tot = tot + jnp.sum(e1, axis=-1, keepdims=True)
-            inv = 1.0 / tot
-            o = _dot((e2 * inv).astype(BF16), r[lo:lo + qb, vcol])
+                tot = tot + jnp.sum(jnp.exp(s1 * scale - ms), axis=-1, keepdims=True)
+            lse = ms + jnp.log(tot)
+            o = _dot(jnp.exp(s2 * scale - lse).astype(BF16), r[lo:lo + qb, vcol])
             if b:
-                o = o + _dot((e1 * inv).astype(BF16), r[0:lo, vcol])
-            r[lo:lo + qb, pl.ds(pl.multiple_of(aw + head * hd, hd), hd)] = o.astype(BF16)
+                o = o + _dot(jnp.exp(s1 * scale - lse).astype(BF16), r[0:lo, vcol])
+            o = o.astype(BF16)
+            for j in range(STACK):
+                col = aw + (kv * group + part * STACK + j) * hd
+                r[lo:lo + qb, pl.ds(pl.multiple_of(col, hd), hd)] = o[j * qb:(j + 1) * qb]
             return cr
 
-        lax.fori_loop(0, cnt, one_head, 0)
+        lax.fori_loop(0, cnt, heads_at, 0)
 
     def o_tile(t):
         slot = t % 2
@@ -326,18 +352,18 @@
 
     def load_gu(t, slot):
         cb = pl.multiple_of(t * tile, tile)
-        return [load_wt(gg, cb, tile, slot, 0), load_wt(gu, cb, tile, slot, 1)]
+        return [load_wt(gu.at[k], cb, tile, slot, k) for k in range(2)]
 
     def fetch_gu(t):
         @pl.when(t % gu_tiles == 0)
         def _():
             wait_sib(pieces_gu(t // gu_tiles))
 
-        for cp in load_gu(t, t % 2):
+        for cp in load_gu(t, (t + 1) % 2):
             cp.start()
 
     def gu_tile(t):
-        slot = t % 2
+        slot = (t + 1) % 2
         for cp in load_gu(t, slot):
             cp.wait()
 
@@ -365,28 +391,31 @@
         cols = pl.ds(pl.multiple_of(t * tile, tile), tile)
         return pltpu.make_async_copy(xb.at[:, cols], out_hbm.at[:, cols], osem.at[2 + t])
 
+    def fetch_d(t):
+        wait_sib(pieces_d(t // dt))
+        load_d(t).start()
+
     def d_item(i):
-        t, mi = i // n_m, i % n_m
+        t, mi = i // n_dm, i % n_dm
 
         @pl.when(mi == 0)
         def _():
-            @pl.when(t % dt == 0)
-            def _():
-                wait_sib(pieces_d(t // dt))
-                load_d(t).start()
-
             @pl.when(t % dt != dt - 1)
             def _():
                 load_d(t + 1).start()
 
             load_d(t).wait()
 
-        m = pl.multiple_of(mi * mb, mb)
-        mm = _dot(r[pl.ds(m, mb), :], wd[t % 2]).astype(BF16).astype(F32)
+        @pl.when((mi == n_dm - 1) & (t % dt == dt - 1) & (t + 1 < n_d))
+        def _():
+            fetch_d(t + 1)
+
+        m = pl.multiple_of(mi * db, db)
+        mm = _dot(r[pl.ds(m, db), :], wd[t % 2]).astype(BF16).astype(F32)
         cols = pl.ds(pl.multiple_of(t * tile, tile), tile)
-        xb[pl.ds(m, mb), cols] = (xb[pl.ds(m, mb), cols].astype(F32) + mm).astype(BF16)
-
-        @pl.when(mi == n_m - 1)
+        xb[pl.ds(m, db), cols] = (xb[pl.ds(m, db), cols].astype(F32) + mm).astype(BF16)
+
+        @pl.when(mi == n_dm - 1)
         def _():
             store_d(t).start()
 
@@ -414,11 +443,19 @@
             def _(b=b):
                 attend(b, w - starts[b])
 
-        @pl.when(w == w_o)
+        @pl.when(w == w_o - 1)
         def _():
             wait_sib(pcs[2:])
             load_wt(go, 0, 512, 0, 0).start()
 
+        @pl.when(w == w_g - 1)
+        def _():
+            fetch_gu(0)
+
+        @pl.when(w == w_d - 1)
+        def _():
+            fetch_d(0)
+
         @pl.when((w >= w_o) & (w < w_g))
         def _():
             o_tile(w - w_o)
@@ -427,7 +464,6 @@
         def _():
             st_k.wait()
             st_v.wait()
-            fetch_gu(0)
             norm(1)
 
         @pl.when((w >= w_g) & (w < w_d))
@@ -472,9 +508,9 @@
         gcol = jnp.pad(jnp.stack([g_attn, g_mlp], axis=1), ((0, 0), (0, 126)))
         wa = jnp.concatenate([w_query, w_key, w_value, gcol], axis=1)
         cos2 = jnp.concatenate([cos_tab, cos_tab], axis=1)
-        sin2 = jnp.concatenate([-sin_tab, sin_tab], axis=1)
+        sin2 = jnp.concatenate([sin_tab, sin_tab], axis=1)
         cfg = (n, ny, rows, drows, dim, ffn, heads, kvh, hd)
-        np_ = 19
+        np_ = 11
         hops = n // 2 - 1
         hbm = pl.BlockSpec(memory_space=pl.ANY)
         sh = jax.ShapeDtypeStruct
@@ -484,10 +520,10 @@
             out_shape=[
                 sh((seq, dim), BF16), sh((seq, kw), BF16), sh((seq, kw), BF16),
                 sh((rows * n, wa.shape[1]), BF16), sh((rows * n, dim), BF16),
-                sh((rows * n, ffn), BF16), sh((rows * n, ffn), BF16), sh((drows * n, dim), BF16),
+                sh((2, rows * n, ffn), BF16), sh((drows * n, dim), BF16),
             ],
             in_specs=[hbm] * 8,
-            out_specs=[hbm] * 8,
+            out_specs=[hbm] * 7,
             scratch_shapes=[
                 pltpu.VMEM((seq, ffn), BF16), pltpu.VMEM((seq, dim), BF16), pltpu.VMEM((seq, dim), BF16),
                 pltpu.VMEM((2, dim, 512), BF16), pltpu.VMEM((2, ffn, 256), BF16),

time: 358 us -> 319 us (0.89)
  Pallas kernels: 339 us -> 301 us
    pallas_call x1, Pallas kernels: 339 us -> 301 us  [local(): pl.pallas_call(functools.partial(layer_kernel, cfg), out_shape=[sh((seq,...]
where the time goes in v2:
time: 319 us
  Pallas kernels  301 us (94%)
  local copies, waits for them, and re-layouts  12.9 us (4%)
  other arithmetic  4.11 us (1%)
    pallas_call x1, Pallas kernels, local(): pl.pallas_call(functools.partial(layer_kernel, cfg), out_shape=[sh((seq,...  301 us
    unnamed x3, local copies, waits for them, and re-layouts  7.34 us

profile of v2, /device:TPU:21, one launch (start us, length us, event | category | flops | bytes accessed | tf_op | source)
XLA Modules:
  0.0 318.9 jit_solution(8881718567822890137)
XLA Ops:
  0.6 0.7 pad_maximum_fusion.2
  1.3 0.1 copy.21
  1.4 1.8 fusion.1.wa_in
  3.2 1.3 copy.22
  4.5 1.3 copy.24
  5.8 1.6 pad_maximum_fusion
  7.4 301.2 %layer.1 = (bf16[1536,1536]{1,0:T(8,128)(2,1)}, bf16[1536,256]{1,0:T(8,128)(2,1)}, bf16[1536,256]{1,0:T(8,128)(2,1)}, bf16[1536,2176]{1,0:T(8,128)(2,1)}, bf16[1...) custom-call(bf16[1536,1536]{1,0:T(8,128)(2,1)} %bitcast.5, ...), custom_call_target="tpu_custom_call" | custom-call | tf_op jit(solution)/shard_map/layer/pallas_call | solution.py:518
  308.6 2.7 reshape.12
  311.4 2.7 reshape.13
  314.1 4.8 %copy.27 = bf16[1,1536,1536]{2,1,0:T(8,128)(2,1)} copy(bf16[1,1536,1536]{2,1,0:T(8,128)(2,1)} %bitcast.4) | data formatting | bytes 9437184
